TPU v7x, 32 devices: a whole 2x2x4 slice. The times are simulated.
32 devices in a mesh: grp: 4 (over y, x), dev: 8 (over z, core).
Axes of the slice: x: 2, y: 2, z: 4, core: 2. Of those that a mesh axis runs over, the one named last changes fastest.
Arguments:
- points: bfloat16 [65536, 256], P(('grp', 'dev')), may hold values from -6 to 6
- ridge: float32 [1024], replicated, may hold values from 0.25 to 2
- landmark_ids: int32 [1024], replicated, may hold values from 0 to 65535, as said below
Outputs:
- features: bfloat16 [65536, 1024], P(('grp', 'dev'))
Inputs may be any that keep to these rules, and one draw needn't show every extreme that they name: `landmark_ids`: sorted ascending, all distinct.
All inputs are finite; a program needn't handle non-finite values.
Results may differ from a plain program's by a relative error of at most 0.0015.
Values may be sent and summed in bfloat16 or wider, within the bound.
No kernel may reach another device: no remote copies, remote signals or barrier semaphores. Data moves between devices by JAX's collectives and lax.ppermute only.
A program may use at most 128 MiB of HBM per device.

v0:
```python
import jax
import jax.numpy as jnp
from jax import lax
from jax.sharding import PartitionSpec as P


def kernel_block(left, right):
    left_sq = jnp.sum(jnp.square(left.astype(jnp.float32)), axis=1)
    right_sq = jnp.sum(jnp.square(right.astype(jnp.float32)), axis=1)
    inner = jnp.dot(left, right.T, preferred_element_type=jnp.float32)
    width = left.shape[1]
    return jnp.exp(-(left_sq[:, None] + right_sq[None, :] - 2.0 * inner) / (2.0 * width))


def shards(points, ridge, landmark_ids):
    count = points.shape[0]
    start = lax.axis_index(("grp", "dev")) * count
    offset = landmark_ids - start
    inside = (offset >= 0) & (offset < count)
    picked = points[jnp.clip(offset, 0, count - 1)]
    filled = jnp.where(inside[:, None], picked.astype(jnp.float32), 0.0)
    marks = lax.psum(filled, ("grp", "dev")).astype(jnp.bfloat16)
    core = kernel_block(marks, marks) + jnp.diag(ridge)
    lower = jnp.linalg.cholesky(core)
    cross = kernel_block(points, marks)
    raw = lax.linalg.triangular_solve(lower, cross, left_side=False, lower=True, transpose_a=True)
    total_rows = count * lax.axis_size(("grp", "dev"))
    totals, squares = lax.psum(
        (jnp.sum(raw, axis=0), jnp.sum(jnp.square(raw), axis=0)), ("grp", "dev")
    )
    mean = totals / total_rows
    var = jnp.maximum(squares / total_rows - jnp.square(mean), 0.0)
    centered = raw - mean[None, :]
    return (centered / jnp.sqrt(var + 1e-05)[None, :]).astype(jnp.bfloat16)


def solution(mesh):
    placed = (P(("grp", "dev"), None), P(), P())
    return jax.shard_map(
        shards, mesh=mesh, in_specs=placed, out_specs=P(("grp", "dev"), None), check_vma=False
    )
```

profile of v0, /device:TPU:0, one launch (start us, length us, event | category | flops | bytes accessed | tf_op | source)
XLA Modules:
  0.0 495.3 jit_solution(2860757767389505931)
XLA Ops:
  3.0 4.9 gather_fusion
  8.1 53.3 %all-reduce.3 = bf16[1024,256]{1,0:T(8,128)(2,1)S(1)} all-reduce(f32[1024,256]{1,0:T(8,128)S(1)} %convert_select_fusion), channel_id=1, replica_groups=mesh['grp'=4,'dev'=8] {'grp','dev'}, use_global_device_ids=true, to_apply=%region_1.2 | all-reduce | flops 262144 | bytes 1572864 | tf_op jit(solution)/shard_map/psum | solution.py:22
  61.6 4.3 fusion.2
  66.0 5.6 %subtract_negate_fusion = (f32[1024,1024]{0,1:T(8,128)}, f32[1024,1024]{0,1:T(8,128)}, f32[1024,1024]{0,1:T(8,128)}) fusion(f32[1024]{0:T(1024)S(1)} %multiply_reduce_fusion.2, bf16[1024,256]{1,0:T(8,128)(2,1)S(1)} %all-reduce.3), kind=kOutput, calls=%fused_computation.27 | convolution fusion | flops 541065216 | bytes 13111296 | tf_op jit(solution)/shard_map/dot_general | solution.py:10
  71.6 5.4 %copy.5 = f32[1024,1024]{1,0:T(8,128)} copy(f32[1024,1024]{0,1:T(8,128)} %get-tuple-element.76) | data formatting | bytes 8388608 | tf_op jit(solution)/shard_map/neg | solution.py:12
  76.9 5.3 %copy.6 = f32[1024,1024]{1,0:T(8,128)} copy(f32[1024,1024]{0,1:T(8,128)} %get-tuple-element.77) | data formatting | bytes 8388608 | tf_op jit(solution)/shard_map/add | solution.py:12
  82.3 6.3 %fusion.16 = f32[1024,1024]{1,0:T(8,128)S(1)} fusion(f32[1024,1024]{1,0:T(8,128)} %copy.6, f32[1024,1024]{1,0:T(8,128)} %copy.5, f32[1024,1024]{0,1:T(8,128)} %get-tuple-element.78, f32[1024]{0:T(1024)S(1)} %copy-done.5), kind=kLoop, calls=%fused_computation.24 | loop fusion | flops 13631488 | bytes 16781312 | tf_op jit(solution)/shard_map/jit(cholesky)/div | solution.py:24
  90.6 11.7 %cholesky.222 = f32[128,128]{1,0:T(8,128)S(1)} custom-call(f32[128,128]{1,0:T(8,128)S(1)} %cholesky.577), custom_call_target="Cholesky" | custom-call | tf_op jit(solution)/shard_map/jit(cholesky)/cholesky | solution.py:24
  102.4 9.8 %custom-call.62 = f32[1,128,128]{1,2,0:T(8,128)S(1)} custom-call(f32[1,128,128]{2,1,0:T(8,128)S(1)} %get-tuple-element.73), custom_call_target="InvertDiagBlocksLowerTriangular" | custom-call | tf_op jit(solution)/shard_map/jit(cholesky)/cholesky | solution.py:24
  118.6 11.7 %cholesky.243 = f32[128,128]{1,0:T(8,128)S(1)} custom-call(f32[128,128]{1,0:T(8,128)S(1)} %cholesky.581), custom_call_target="Cholesky" | custom-call | tf_op jit(solution)/shard_map/jit(cholesky)/cholesky | solution.py:24
  132.9 10.2 %custom-call.63 = f32[1,128,128]{1,2,0:T(8,128)S(1)} custom-call(f32[1,128,128]{2,1,0:T(8,128)S(1)} %get-tuple-element.70), custom_call_target="InvertDiagBlocksLowerTriangular" | custom-call | tf_op jit(solution)/shard_map/jit(cholesky)/cholesky | solution.py:24
  146.4 11.7 %cholesky.466 = f32[128,128]{1,0:T(8,128)S(1)} custom-call(f32[128,128]{1,0:T(8,128)S(1)} %cholesky.586), custom_call_target="Cholesky" | custom-call | tf_op jit(solution)/shard_map/jit(cholesky)/cholesky | solution.py:24
  160.1 9.8 %custom-call.64 = f32[1,128,128]{1,2,0:T(8,128)S(1)} custom-call(f32[1,128,128]{2,1,0:T(8,128)S(1)} %get-tuple-element.67), custom_call_target="InvertDiagBlocksLowerTriangular" | custom-call | tf_op jit(solution)/shard_map/jit(cholesky)/cholesky | solution.py:24
  173.4 11.9 %cholesky.485 = f32[128,128]{1,0:T(8,128)S(1)} custom-call(f32[128,128]{1,0:T(8,128)S(1)} %cholesky.591), custom_call_target="Cholesky" | custom-call | tf_op jit(solution)/shard_map/jit(cholesky)/cholesky | solution.py:24
  187.2 9.8 %custom-call.65 = f32[1,128,128]{1,2,0:T(8,128)S(1)} custom-call(f32[1,128,128]{2,1,0:T(8,128)S(1)} %get-tuple-element.64), custom_call_target="InvertDiagBlocksLowerTriangular" | custom-call | tf_op jit(solution)/shard_map/jit(cholesky)/cholesky | solution.py:24
  200.4 11.7 %cholesky.504 = f32[128,128]{1,0:T(8,128)S(1)} custom-call(f32[128,128]{1,0:T(8,128)S(1)} %cholesky.596), custom_call_target="Cholesky" | custom-call | tf_op jit(solution)/shard_map/jit(cholesky)/cholesky | solution.py:24
  214.0 9.8 %custom-call.66 = f32[1,128,128]{1,2,0:T(8,128)S(1)} custom-call(f32[1,128,128]{2,1,0:T(8,128)S(1)} %get-tuple-element.61), custom_call_target="InvertDiagBlocksLowerTriangular" | custom-call | tf_op jit(solution)/shard_map/jit(cholesky)/cholesky | solution.py:24
  227.4 11.7 %cholesky.524 = f32[128,128]{1,0:T(8,128)S(1)} custom-call(f32[128,128]{1,0:T(8,128)S(1)} %cholesky.601), custom_call_target="Cholesky" | custom-call | tf_op jit(solution)/shard_map/jit(cholesky)/cholesky | solution.py:24
  241.0 9.8 %custom-call.67 = f32[1,128,128]{1,2,0:T(8,128)S(1)} custom-call(f32[1,128,128]{2,1,0:T(8,128)S(1)} %get-tuple-element.58), custom_call_target="InvertDiagBlocksLowerTriangular" | custom-call | tf_op jit(solution)/shard_map/jit(cholesky)/cholesky | solution.py:24
  253.9 11.7 %cholesky.544 = f32[128,128]{1,0:T(8,128)S(1)} custom-call(f32[128,128]{1,0:T(8,128)S(1)} %cholesky.606), custom_call_target="Cholesky" | custom-call | tf_op jit(solution)/shard_map/jit(cholesky)/cholesky | solution.py:24
  267.5 10.2 %custom-call.68 = f32[1,128,128]{1,2,0:T(8,128)S(1)} custom-call(f32[1,128,128]{2,1,0:T(8,128)S(1)} %get-tuple-element.55), custom_call_target="InvertDiagBlocksLowerTriangular" | custom-call | tf_op jit(solution)/shard_map/jit(cholesky)/cholesky | solution.py:24
  280.4 11.7 %cholesky.562 = f32[128,128]{1,0:T(8,128)S(1)} custom-call(f32[128,128]{1,0:T(8,128)S(1)} %convolution_subtract_fusion.11), custom_call_target="Cholesky" | custom-call | tf_op jit(solution)/shard_map/jit(cholesky)/cholesky | solution.py:24
  293.9 4.9 select_select_fusion
  298.8 22.5 %while.1 = (s32[]{:T(128)}, f32[1024,1024]{1,0:T(8,128)}, s32[8,2]{0,1:T(2,128)S(1)}, f32[8,128,128]{2,1,0:T(8,128)S(1)}, s32[]{:T(128)}) while((s32[]{:T(128)}, f32[1024,1024]{1,0:T(8,128)}, s32[8,2]{0,1:T(2,128)S(1)}, f32[8,128,128]{2,1,0:T(8,128)S(1)}, s32[]{:T(128)}) %tuple.61), condition=%wide.while_cond, body=%wide.while_body.sunk | while | flops 2 | bytes 131189 | solution.py:26
  321.2 78.8 %custom-call.69 = f32[8,128,128]{1,2,0:T(8,128)S(1)} custom-call(f32[8,128,128]{2,1,0:T(8,128)S(1)} %get-tuple-element.12), custom_call_target="InvertDiagBlocksLowerTriangular" | custom-call | tf_op jit(solution)/shard_map/triangular_solve | solution.py:26
  415.6 5.0 %fusion.26 = f32[2048,128]{0,1:T(8,128)} fusion(f32[2048,128]{0,1:T(8,128)} %get-tuple-element.84, f32[2048,128]{0,1:T(8,128)S(1)} %get-tuple-element.83, f32[2048,128]{0,1:T(8,128)S(1)} %get-tuple-element.82, f32[2048,128]{0,1:T(8,128)S(1)} %get-tuple-element.81, f32[2048,1024]{0,1:T(8,128)S(1)} %bitcast.124, f32[1024,1024]{1,0:T(8,128)} %get-tuple-element.131), kind=kOutput, calls=%fused_computation.42 | convolution fusion | flops 1614020608 | bytes 6553600 | tf_op jit(solution)/shard_map/triangular_solve | solution.py:26
  423.0 4.3 convolution_subtract_fusion.2
  428.5 4.6 convolution_subtract_fusion
  434.2 5.8 %convolution_subtract_fusion.1 = f32[2048,128]{0,1:T(8,128)S(1)} fusion(f32[2048,896]{0,1:T(8,128)S(1)} %get-tuple-element.27, f32[2048,1024]{0,1:T(8,128)S(1)} %bitcast.124, f32[1024,1024]{1,0:T(8,128)} %get-tuple-element.131), kind=kOutput, calls=%fused_computation.38 | convolution fusion | flops 2818834432 | bytes 9895936 | tf_op jit(solution)/shard_map/triangular_solve | solution.py:26
  444.3 38.9 %all-reduce.1 = (f32[1024]{0:T(1024)S(1)}, f32[1024]{0:T(1024)S(1)}) all-reduce(f32[1024]{0:T(1024)S(1)} %get-tuple-element.14, f32[1024]{0:T(1024)S(1)} %get-tuple-element.13), channel_id=1, replica_groups=mesh['grp'=4,'dev'=8] {'grp','dev'}, use_global_device_ids=true, to_apply=%region_22.23 | all-reduce | flops 2048 | bytes 16384 | tf_op jit(solution)/shard_map/psum | solution.py:28
  483.1 5.3 %divide_convert_fusion = bf16[2048,1024]{0,1:T(8,128)(2,1)} fusion(f32[2048,1024]{0,1:T(8,128)} %copy-done, f32[1024]{0:T(1024)S(1)} %get-tuple-element.75, f32[1024]{0:T(1024)S(1)} %get-tuple-element.74), kind=kLoop, calls=%fused_computation.7 | loop fusion | flops 6291456 | bytes 12591104 | tf_op jit(solution)/shard_map/convert_element_type | solution.py:34
  488.5 6.4 %copy.7 = bf16[2048,1024]{1,0:T(8,128)(2,1)} copy(bf16[2048,1024]{0,1:T(8,128)(2,1)} %divide_convert_fusion) | data formatting | bytes 8388608 | tf_op jit(solution)/shard_map/convert_element_type | solution.py:34
  (99 shorter events, 87.1 us)
Async XLA Ops:
  3.0 58.6 %copy-start.1 = (bf16[2048,256]{1,0:T(8,128)(2,1)S(1)}, bf16[2048,256]{1,0:T(8,128)(2,1)}, u32[]{:S(2)}) copy-start(bf16[2048,256]{1,0:T(8,128)(2,1)} %param.3) | copy-start | bytes 3145732
  76.9 5.4 %copy-start.5 = (f32[1024]{0:T(1024)S(1)}, f32[1024]{0:T(1024)}, u32[]{:S(2)}) copy-start(f32[1024]{0:T(1024)} %param.4) | copy-start | bytes 12292
  88.6 2.0 copy-start.2
  400.0 5.3 %copy-start.3 = (f32[8,128,128]{1,2,0:T(8,128)}, f32[8,128,128]{1,2,0:T(8,128)S(1)}, u32[]{:S(2)}) copy-start(f32[8,128,128]{1,2,0:T(8,128)S(1)} %custom-call.69) | copy-start | bytes 1572868
  400.0 6.6 %slice-start = ((s8[8388608]{0:T(1024)(128)(4,1)}), s8[4194304]{0:T(1024)(128)(4,1)S(1)}, s32[]{:S(2)}) async-start(s8[8388608]{0:T(1024)(128)(4,1)} %bitcast.123), calls=%async_computation | async-start | bytes 8388608
  402.8 3.8 slice-start.1
  406.6 2.3 copy-start.4
  441.0 3.2 copy-start
where the time goes:
time: 502 us; the launch traced here: 495 us
  other arithmetic  272 us (54%)
  blocking collectives  92.1 us (18%)
  matrix products  74 us (15%)
  local copies, waits for them, and re-layouts  51 us (10%)
  between operations  5.8 us (1%)
    another operation x30, other arithmetic, shards(): lower = jnp.linalg.cholesky(core)  172 us
    another operation x3, other arithmetic, shards(): lax.linalg.triangular_solve(lower, cross, left_side=False, lower=True, tr...  83.7 us
    psum x1, blocking collectives, shards(): marks = lax.psum(filled, ('grp', 'dev')).astype(jnp.bfloat16)  53.3 us
    another operation x15, matrix products, shards(): lax.linalg.triangular_solve(lower, cross, left_side=False, lower=True, tr...  40.8 us
    psum x1, blocking collectives, shards(): lax.psum((jnp.sum(raw, axis=0), jnp.sum(jnp.square(raw), axis=0)), ('grp'...  38.9 us
    another operation x14, matrix products, shards(): lower = jnp.linalg.cholesky(core)  23.2 us
    another operation x24, local copies, waits for them, and re-layouts  22.3 us

commit v1 on v0

--- a/solution.py
+++ b/solution.py
@@ -26,7 +26,7 @@
     raw = lax.linalg.triangular_solve(lower, cross, left_side=False, lower=True, transpose_a=True)
     total_rows = count * lax.axis_size(("grp", "dev"))
     totals, squares = lax.psum(
-        (jnp.sum(raw, axis=0), jnp.sum(jnp.square(raw), axis=0)), ("grp", "dev")
+        lax.psum((jnp.sum(raw, axis=0), jnp.sum(jnp.square(raw), axis=0)), "dev"), "grp"
     )
     mean = totals / total_rows
     var = jnp.maximum(squares / total_rows - jnp.square(mean), 0.0)

time: 502 us -> 486 us (0.968)
  blocking collectives: 92.1 us -> 76.2 us
    psum x1 -> x2, blocking collectives: 38.9 us -> 22.9 us  [the longest x1 13.8 us: shards(): lax.psum((jnp.sum(raw, axis=0), jnp.sum(jnp.square(raw), axis=0)), 'dev')]
where the time goes in v1:
time: 486 us; the launch traced here: 479 us
  other arithmetic  272 us (56%)
  blocking collectives  76.2 us (16%)
  matrix products  74 us (15%)
  local copies, waits for them, and re-layouts  51 us (10%)
  between operations  5.82 us (1%)
    another operation x30, other arithmetic, shards(): lower = jnp.linalg.cholesky(core)  172 us
    another operation x3, other arithmetic, shards(): lax.linalg.triangular_solve(lower, cross, left_side=False, lower=True, tr...  83.7 us
    psum x1, blocking collectives, shards(): marks = lax.psum(filled, ('grp', 'dev')).astype(jnp.bfloat16)  53.3 us
    another operation x15, matrix products, shards(): lax.linalg.triangular_solve(lower, cross, left_side=False, lower=True, tr...  40.8 us
    another operation x14, matrix products, shards(): lower = jnp.linalg.cholesky(core)  23.2 us
    another operation x24, local copies, waits for them, and re-layouts  22.3 us
    psum x1, blocking collectives, shards(): lax.psum((jnp.sum(raw, axis=0), jnp.sum(jnp.square(raw), axis=0)), 'dev')  13.8 us
    dot_general x2, matrix products, kernel_block(): inner = jnp.dot(left, right.T, preferred_element_type=jnp.float32)  9.96 us

profile of v1, /device:TPU:0, one launch (start us, length us, event | category | flops | bytes accessed | tf_op | source)
XLA Modules:
  0.0 479.4 jit_solution(18303198051235936058)
XLA Ops:
  3.0 4.9 %gather_fusion = bf16[1024,256]{1,0:T(8,128)(2,1)S(1)} fusion(bf16[2048,256]{1,0:T(8,128)(2,1)} %param.3, s32[1024]{0:T(1024)S(1)} %fusion.74), kind=kCustom, calls=%fused_computation | custom fusion | bytes 1052672 | tf_op jit(solution)/shard_map/gather | solution.py:20
  8.1 53.3 %all-reduce.4 = bf16[1024,256]{1,0:T(8,128)(2,1)S(1)} all-reduce(f32[1024,256]{1,0:T(8,128)S(1)} %convert_select_fusion), channel_id=1, replica_groups=mesh['grp'=4,'dev'=8] {'grp','dev'}, use_global_device_ids=true, to_apply=%region_1.2 | all-reduce | flops 262144 | bytes 1572864 | tf_op jit(solution)/shard_map/psum | solution.py:22
  61.6 4.3 fusion.2
  66.0 5.6 %subtract_negate_fusion = (f32[1024,1024]{0,1:T(8,128)}, f32[1024,1024]{0,1:T(8,128)}, f32[1024,1024]{0,1:T(8,128)}) fusion(f32[1024]{0:T(1024)S(1)} %multiply_reduce_fusion.2, bf16[1024,256]{1,0:T(8,128)(2,1)S(1)} %all-reduce.4), kind=kOutput, calls=%fused_computation.27 | convolution fusion | flops 541065216 | bytes 13111296 | tf_op jit(solution)/shard_map/dot_general | solution.py:10
  71.6 5.4 %copy.5 = f32[1024,1024]{1,0:T(8,128)} copy(f32[1024,1024]{0,1:T(8,128)} %get-tuple-element.78) | data formatting | bytes 8388608 | tf_op jit(solution)/shard_map/neg | solution.py:12
  76.9 5.3 %copy.6 = f32[1024,1024]{1,0:T(8,128)} copy(f32[1024,1024]{0,1:T(8,128)} %get-tuple-element.79) | data formatting | bytes 8388608 | tf_op jit(solution)/shard_map/add | solution.py:12
  82.3 6.3 %fusion.16 = f32[1024,1024]{1,0:T(8,128)S(1)} fusion(f32[1024,1024]{1,0:T(8,128)} %copy.6, f32[1024,1024]{1,0:T(8,128)} %copy.5, f32[1024,1024]{0,1:T(8,128)} %get-tuple-element.80, f32[1024]{0:T(1024)S(1)} %copy-done.5), kind=kLoop, calls=%fused_computation.24 | loop fusion | flops 13631488 | bytes 16781312 | tf_op jit(solution)/shard_map/jit(cholesky)/div | solution.py:24
  90.6 11.7 %cholesky.222 = f32[128,128]{1,0:T(8,128)S(1)} custom-call(f32[128,128]{1,0:T(8,128)S(1)} %cholesky.577), custom_call_target="Cholesky" | custom-call | tf_op jit(solution)/shard_map/jit(cholesky)/cholesky | solution.py:24
  102.4 9.8 %custom-call.62 = f32[1,128,128]{1,2,0:T(8,128)S(1)} custom-call(f32[1,128,128]{2,1,0:T(8,128)S(1)} %get-tuple-element.75), custom_call_target="InvertDiagBlocksLowerTriangular" | custom-call | tf_op jit(solution)/shard_map/jit(cholesky)/cholesky | solution.py:24
  118.6 11.7 %cholesky.243 = f32[128,128]{1,0:T(8,128)S(1)} custom-call(f32[128,128]{1,0:T(8,128)S(1)} %cholesky.581), custom_call_target="Cholesky" | custom-call | tf_op jit(solution)/shard_map/jit(cholesky)/cholesky | solution.py:24
  132.9 10.2 %custom-call.63 = f32[1,128,128]{1,2,0:T(8,128)S(1)} custom-call(f32[1,128,128]{2,1,0:T(8,128)S(1)} %get-tuple-element.72), custom_call_target="InvertDiagBlocksLowerTriangular" | custom-call | tf_op jit(solution)/shard_map/jit(cholesky)/cholesky | solution.py:24
  146.4 11.7 %cholesky.466 = f32[128,128]{1,0:T(8,128)S(1)} custom-call(f32[128,128]{1,0:T(8,128)S(1)} %cholesky.586), custom_call_target="Cholesky" | custom-call | tf_op jit(solution)/shard_map/jit(cholesky)/cholesky | solution.py:24
  160.1 9.8 %custom-call.64 = f32[1,128,128]{1,2,0:T(8,128)S(1)} custom-call(f32[1,128,128]{2,1,0:T(8,128)S(1)} %get-tuple-element.69), custom_call_target="InvertDiagBlocksLowerTriangular" | custom-call | tf_op jit(solution)/shard_map/jit(cholesky)/cholesky | solution.py:24
  173.4 11.9 %cholesky.485 = f32[128,128]{1,0:T(8,128)S(1)} custom-call(f32[128,128]{1,0:T(8,128)S(1)} %cholesky.591), custom_call_target="Cholesky" | custom-call | tf_op jit(solution)/shard_map/jit(cholesky)/cholesky | solution.py:24
  187.2 9.8 %custom-call.65 = f32[1,128,128]{1,2,0:T(8,128)S(1)} custom-call(f32[1,128,128]{2,1,0:T(8,128)S(1)} %get-tuple-element.66), custom_call_target="InvertDiagBlocksLowerTriangular" | custom-call | tf_op jit(solution)/shard_map/jit(cholesky)/cholesky | solution.py:24
  200.4 11.7 %cholesky.504 = f32[128,128]{1,0:T(8,128)S(1)} custom-call(f32[128,128]{1,0:T(8,128)S(1)} %cholesky.596), custom_call_target="Cholesky" | custom-call | tf_op jit(solution)/shard_map/jit(cholesky)/cholesky | solution.py:24
  214.0 9.8 %custom-call.66 = f32[1,128,128]{1,2,0:T(8,128)S(1)} custom-call(f32[1,128,128]{2,1,0:T(8,128)S(1)} %get-tuple-element.63), custom_call_target="InvertDiagBlocksLowerTriangular" | custom-call | tf_op jit(solution)/shard_map/jit(cholesky)/cholesky | solution.py:24
  227.4 11.7 %cholesky.524 = f32[128,128]{1,0:T(8,128)S(1)} custom-call(f32[128,128]{1,0:T(8,128)S(1)} %cholesky.601), custom_call_target="Cholesky" | custom-call | tf_op jit(solution)/shard_map/jit(cholesky)/cholesky | solution.py:24
  241.0 9.8 %custom-call.67 = f32[1,128,128]{1,2,0:T(8,128)S(1)} custom-call(f32[1,128,128]{2,1,0:T(8,128)S(1)} %get-tuple-element.60), custom_call_target="InvertDiagBlocksLowerTriangular" | custom-call | tf_op jit(solution)/shard_map/jit(cholesky)/cholesky | solution.py:24
  253.9 11.7 %cholesky.544 = f32[128,128]{1,0:T(8,128)S(1)} custom-call(f32[128,128]{1,0:T(8,128)S(1)} %cholesky.606), custom_call_target="Cholesky" | custom-call | tf_op jit(solution)/shard_map/jit(cholesky)/cholesky | solution.py:24
  267.5 10.2 %custom-call.68 = f32[1,128,128]{1,2,0:T(8,128)S(1)} custom-call(f32[1,128,128]{2,1,0:T(8,128)S(1)} %get-tuple-element.57), custom_call_target="InvertDiagBlocksLowerTriangular" | custom-call | tf_op jit(solution)/shard_map/jit(cholesky)/cholesky | solution.py:24
  280.3 11.7 %cholesky.562 = f32[128,128]{1,0:T(8,128)S(1)} custom-call(f32[128,128]{1,0:T(8,128)S(1)} %convolution_subtract_fusion.11), custom_call_target="Cholesky" | custom-call | tf_op jit(solution)/shard_map/jit(cholesky)/cholesky | solution.py:24
  293.9 4.9 %select_select_fusion = f32[1024,1024]{1,0:T(8,128)} fusion(f32[1024,1024]{1,0:T(8,128)} %get-tuple-element.55, pred[]{:T(512)S(6)} %cholesky.576), kind=kLoop, calls=%fused_computation.9 | loop fusion | flops 4194304 | bytes 8388609 | tf_op jit(solution)/shard_map/triangular_solve | solution.py:26
  298.8 22.5 %while.1 = (s32[]{:T(128)}, f32[1024,1024]{1,0:T(8,128)}, s32[8,2]{0,1:T(2,128)S(1)}, f32[8,128,128]{2,1,0:T(8,128)S(1)}, s32[]{:T(128)}) while((s32[]{:T(128)}, f32[1024,1024]{1,0:T(8,128)}, s32[8,2]{0,1:T(2,128)S(1)}, f32[8,128,128]{2,1,0:T(8,128)S(1)}, s32[]{:T(128)}) %tuple.61), condition=%wide.while_cond, body=%wide.while_body.sunk | while | flops 2 | bytes 131189 | solution.py:26
  321.2 78.8 %custom-call.69 = f32[8,128,128]{1,2,0:T(8,128)S(1)} custom-call(f32[8,128,128]{2,1,0:T(8,128)S(1)} %get-tuple-element.12), custom_call_target="InvertDiagBlocksLowerTriangular" | custom-call | tf_op jit(solution)/shard_map/triangular_solve | solution.py:26
  415.6 5.0 %fusion.26 = f32[2048,128]{0,1:T(8,128)} fusion(f32[2048,128]{0,1:T(8,128)} %get-tuple-element.86, f32[2048,128]{0,1:T(8,128)S(1)} %get-tuple-element.85, f32[2048,128]{0,1:T(8,128)S(1)} %get-tuple-element.84, f32[2048,128]{0,1:T(8,128)S(1)} %get-tuple-element.83, f32[2048,1024]{0,1:T(8,128)S(1)} %bitcast.124, f32[1024,1024]{1,0:T(8,128)} %get-tuple-element.133), kind=kOutput, calls=%fused_computation.42 | convolution fusion | flops 1614020608 | bytes 6553600 | tf_op jit(solution)/shard_map/triangular_solve | solution.py:26
  428.5 4.6 convolution_subtract_fusion
  434.2 5.8 %convolution_subtract_fusion.1 = f32[2048,128]{0,1:T(8,128)S(1)} fusion(f32[2048,896]{0,1:T(8,128)S(1)} %get-tuple-element.29, f32[2048,1024]{0,1:T(8,128)S(1)} %bitcast.124, f32[1024,1024]{1,0:T(8,128)} %get-tuple-element.133), kind=kOutput, calls=%fused_computation.38 | convolution fusion | flops 2818834432 | bytes 9895936 | tf_op jit(solution)/shard_map/triangular_solve | solution.py:26
  444.3 13.8 %all-reduce.1 = (f32[1024]{0:T(1024)S(1)}, f32[1024]{0:T(1024)S(1)}) all-reduce(f32[1024]{0:T(1024)S(1)} %get-tuple-element.14, f32[1024]{0:T(1024)S(1)} %get-tuple-element.13), channel_id=1, replica_groups=mesh['grp'=4,'dev'=8] {'dev'}, use_global_device_ids=true, to_apply=%region_23.24 | all-reduce | flops 2048 | bytes 16384 | tf_op jit(solution)/shard_map/psum | solution.py:29
  458.1 9.1 %all-reduce.2 = (f32[1024]{0:T(1024)S(1)}, f32[1024]{0:T(1024)S(1)}) all-reduce(f32[1024]{0:T(1024)S(1)} %get-tuple-element.23, f32[1024]{0:T(1024)S(1)} %get-tuple-element.24), channel_id=1, replica_groups=mesh['grp'=4,'dev'=8] {'grp'}, use_global_device_ids=true, to_apply=%region_24.25 | all-reduce | flops 2048 | bytes 16384 | tf_op jit(solution)/shard_map/psum | solution.py:28
  467.2 5.3 %divide_convert_fusion = bf16[2048,1024]{0,1:T(8,128)(2,1)} fusion(f32[2048,1024]{0,1:T(8,128)} %copy-done, f32[1024]{0:T(1024)S(1)} %get-tuple-element.77, f32[1024]{0:T(1024)S(1)} %get-tuple-element.76), kind=kLoop, calls=%fused_computation.7 | loop fusion | flops 6291456 | bytes 12591104 | tf_op jit(solution)/shard_map/convert_element_type | solution.py:34
  472.5 6.4 %copy.7 = bf16[2048,1024]{1,0:T(8,128)(2,1)} copy(bf16[2048,1024]{0,1:T(8,128)(2,1)} %divide_convert_fusion) | data formatting | bytes 8388608 | tf_op jit(solution)/shard_map/convert_element_type | solution.py:34
  (100 shorter events, 91.4 us)
Async XLA Ops:
  3.0 58.6 %copy-start.1 = (bf16[2048,256]{1,0:T(8,128)(2,1)S(1)}, bf16[2048,256]{1,0:T(8,128)(2,1)}, u32[]{:S(2)}) copy-start(bf16[2048,256]{1,0:T(8,128)(2,1)} %param.3) | copy-start | bytes 3145732
  76.9 5.4 %copy-start.5 = (f32[1024]{0:T(1024)S(1)}, f32[1024]{0:T(1024)}, u32[]{:S(2)}) copy-start(f32[1024]{0:T(1024)} %param.4) | copy-start | bytes 12292
  88.6 2.0 copy-start.2
  400.0 5.3 %copy-start.3 = (f32[8,128,128]{1,2,0:T(8,128)}, f32[8,128,128]{1,2,0:T(8,128)S(1)}, u32[]{:S(2)}) copy-start(f32[8,128,128]{1,2,0:T(8,128)S(1)} %custom-call.69) | copy-start | bytes 1572868
  400.0 6.6 %slice-start = ((s8[8388608]{0:T(1024)(128)(4,1)}), s8[4194304]{0:T(1024)(128)(4,1)S(1)}, s32[]{:S(2)}) async-start(s8[8388608]{0:T(1024)(128)(4,1)} %bitcast.123), calls=%async_computation | async-start | bytes 8388608
  402.8 3.8 slice-start.1
  406.6 2.3 copy-start.4
  441.0 3.2 copy-start
